TPU v7x, 32 devices: a whole 2x2x4 slice. The times are simulated.
32 devices in a mesh: blk: 8 (over z, y), grp: 4 (over x, core).
Axes of the slice: x: 2, y: 2, z: 4, core: 2. Of those that a mesh axis runs over, the one named last changes fastest.
Arguments:
- start_state: float32 [64, 4096], P(('blk', 'grp')), may hold values from -6 to 6
- start_log_weight: float32 [64], P(('blk', 'grp')), may hold values from -10 to 330
- noise: bfloat16 [3, 64, 4096], P(None, ('blk', 'grp')), may hold values from -6 to 6
- first_weight: bfloat16 [14336, 4096], P('blk'), may hold values from -0.09375 to 0.09375
- second_weight: bfloat16 [14336, 4096], P('blk'), may hold values from -0.09375 to 0.09375
- third_weight: bfloat16 [14336, 4096], P('blk'), may hold values from -0.09375 to 0.09375
Outputs:
- final_state: float32 [64, 4096], P(('blk', 'grp'))
- log_weight: float32 [64], P(('blk', 'grp'))
- log_ratio: float32 [], replicated
All inputs are finite; a program needn't handle non-finite values.
Results may differ from a plain program's by a relative error of at most 0.00074.
Values may be sent and summed in bfloat16 or wider, within the bound.
No kernel may reach another device: no remote copies, remote signals or barrier semaphores. Data moves between devices by JAX's collectives and lax.ppermute only.
A program may use at most 128 MiB of HBM per device.

v0:
```python
import functools
import math

import jax
import jax.numpy as jnp
from jax import lax
from jax.experimental import pallas as pl
from jax.experimental.pallas import tpu as pltpu
from jax.sharding import Mesh
from jax.sharding import PartitionSpec as P

LANES = 128


def chunk_rows(rows):
    return 128 if rows % 128 == 0 else rows


def column_tile(columns):
    return 512 if columns % 512 == 0 else columns


def lane_width(count):
    return -(-count // LANES) * LANES


def as_row(column, width):
    spread = jnp.broadcast_to(column, (column.shape[0], LANES))
    spread = jnp.pad(spread, ((0, width - column.shape[0]), (0, 0)))
    return spread.T[:1, :]


def paired(first, second, rows):
    shape = (rows, first.shape[1])
    odd = lax.broadcasted_iota(jnp.int32, shape, 0) % 2 == 1
    return jnp.where(odd, jnp.broadcast_to(second, shape), jnp.broadcast_to(first, shape))


def step_kernel(
    mine_ref, other_ref, base_ref, w1_ref, w2_ref, w3_ref,
    mine_out, other_out, next_base, held, factors, sems, *, last, steps,
):
    hidden, columns = held.shape[1], held.shape[2]
    near = mine_ref.shape[0]
    chunk = chunk_rows(hidden)
    start = lax.axis_index("half") * hidden
    sources = (w1_ref, w2_ref, w3_ref)
    copies = []
    for j in range(hidden // chunk):
        for i in range(3):
            copy = pltpu.make_async_copy(
                sources[i].at[pl.ds(pl.multiple_of(start + j * chunk, 16), chunk)],
                held.at[i, pl.ds(j * chunk, chunk)],
                sems.at[j, i],
            )
            copy.start()
            copies.append(copy)
    state = jnp.concatenate([mine_ref[...], other_ref[...]], axis=0)
    contract = (((1,), (1,)), ((), ()))
    energy = jnp.zeros((state.shape[0], 1), jnp.float32)
    for j in range(hidden // chunk):
        rows = pl.ds(j * chunk, chunk)
        pre = []
        for i in range(3):
            copies[3 * j + i].wait()
        for i in range(3):
            pre.append(
                lax.dot_general(state, held[i, rows], contract, preferred_element_type=jnp.float32)
            )
        pre_a, pre_b, pre_c = pre
        decay = jnp.exp(-jnp.abs(pre_a))
        soft = jnp.maximum(pre_a, 0.0) + jnp.log1p(decay)
        sigma = jnp.where(pre_a >= 0.0, 1.0, decay) / (1.0 + decay)
        tan_b = jnp.tanh(pre_b)
        soft_tan = soft * tan_b
        energy = energy + jnp.sum(soft_tan * pre_c, axis=1, keepdims=True)
        factors[0, :, rows] = (sigma * tan_b * pre_c).astype(jnp.bfloat16)
        factors[1, :, rows] = (soft * (1.0 - tan_b * tan_b) * pre_c).astype(jnp.bfloat16)
        factors[2, :, rows] = soft_tan.astype(jnp.bfloat16)
    width = base_ref.shape[1]
    shift = energy / steps
    mine_row = base_ref[0:1, :] - as_row(shift[:near], width)
    other_row = base_ref[1:2, :] - as_row(shift[near:], width)
    if last:
        mine_out[:, columns:] = paired(mine_row, other_row, near)
        other_out[:, columns:] = paired(other_row, mine_row, near)
    next_base[...] = paired(mine_row, other_row, 8)
    tile = column_tile(columns)
    for j in range(columns // tile):
        cols = pl.ds(j * tile, tile)
        total = jnp.dot(factors[0], held[0, :, cols], preferred_element_type=jnp.float32)
        total = total + jnp.dot(factors[1], held[1, :, cols], preferred_element_type=jnp.float32)
        total = total + jnp.dot(factors[2], held[2, :, cols], preferred_element_type=jnp.float32)
        mine_out[:, cols] = total[:near]
        other_out[:, cols] = total[near:]


def head_step(mine, other, base, weights, hidden, last, steps):
    near, columns = mine.shape
    width = base.shape[1]
    chunk = chunk_rows(hidden)
    wide = columns + width if last else columns
    vmem = pl.BlockSpec(memory_space=pltpu.VMEM)
    return pl.pallas_call(
        functools.partial(step_kernel, last=last, steps=steps),
        out_shape=(
            jax.ShapeDtypeStruct((near, wide), jnp.float32),
            jax.ShapeDtypeStruct((near, wide), jnp.float32),
            jax.ShapeDtypeStruct((8, width), jnp.float32),
        ),
        in_specs=[vmem] * 3 + [pl.BlockSpec(memory_space=pl.ANY)] * 3,
        out_specs=(vmem,) * 3,
        scratch_shapes=[
            pltpu.VMEM((3, hidden, columns), jnp.bfloat16),
            pltpu.VMEM((3, 2 * near, hidden), jnp.bfloat16),
            pltpu.SemaphoreType.DMA((hidden // chunk, 3)),
        ],
        compiler_params=pltpu.CompilerParams(vmem_limit_bytes=40 * 1024 * 1024),
        cost_estimate=pl.CostEstimate(
            flops=24 * near * hidden * columns,
            bytes_accessed=6 * hidden * columns,
            transcendentals=8 * near * hidden,
        ),
        name="head_step",
    )(mine, other, base, *weights)


def per_device(start_state, start_log_weight, noise, first_weight, second_weight, third_weight):
    steps = noise.shape[0]
    own, columns = start_state.shape
    weights = (first_weight, second_weight, third_weight)
    peers, halves, planes = lax.axis_size("blk"), lax.axis_size("half"), lax.axis_size("side")
    assert halves == 2
    hidden = first_weight.shape[0] // halves
    near = peers * own
    width = lane_width(near)
    at = lax.axis_index("blk") * own

    def exchange(value):
        return lax.all_to_all(value, "blk", 0, 0, tiled=True)

    def swap(value):
        return lax.ppermute(value, "half", [(0, 1), (1, 0)])

    base = lax.dynamic_update_slice(jnp.zeros((8, width), jnp.float32), start_log_weight[None], (0, at))
    state = start_state
    for step in range(steps):
        last = step == steps - 1
        rounded = state.astype(jnp.bfloat16)
        mine = exchange(jnp.broadcast_to(rounded[None], (peers, own, columns))).reshape(near, columns)
        other = swap(mine)
        mine_part, other_part, base = head_step(mine, other, base, weights, hidden, last, steps)
        part = mine_part + swap(other_part)
        got = jnp.sum(exchange(part.reshape(peers, own, part.shape[1])), axis=0)
        gradient = got[:, :columns]
        beta = (step + 1) / steps
        state = (
            state
            - 0.05 * (state + beta * gradient)
            + math.sqrt(0.1) * noise[step].astype(jnp.float32)
        )
    plane = got[:, columns : columns + near]
    log_weight = lax.dynamic_slice_in_dim(plane[0], at, own, 0)
    top = jnp.max(plane)
    total = jnp.sum(jnp.exp(plane - top))
    pair = jnp.stack([top, total])
    pairs = [pair]
    for shift in range(1, planes):
        pairs.append(lax.ppermute(pair, "side", [(a, (a + shift) % planes) for a in range(planes)]))
    tops = jnp.stack([p[0] for p in pairs])
    totals = jnp.stack([p[1] for p in pairs])
    top = jnp.max(tops)
    total = jnp.sum(totals * jnp.exp(tops - top))
    log_ratio = top + jnp.log(total) - math.log(near * halves * planes)
    return (state, log_weight, log_ratio)


def solution(mesh):
    blk, grp = mesh.shape["blk"], mesh.shape["grp"]
    fine = Mesh(mesh.devices.reshape(blk, grp // 2, 2), ("blk", "side", "half"))
    every = ("blk", "side", "half")
    placed = (
        P(every, None),
        P(every),
        P(None, every, None),
        P("blk", None),
        P("blk", None),
        P("blk", None),
    )
    return jax.shard_map(
        per_device,
        mesh=fine,
        in_specs=placed,
        out_specs=(P(every, None), P(every), P()),
        check_vma=False,
    )
```

profile of v0, /device:TPU:0, one launch (start us, length us, event | category | flops | bytes accessed | tf_op | source)
XLA Modules:
  0.0 146.6 jit_solution(12857102262994933993)
XLA Ops:
  0.6 0.8 convert_element_type.21
  1.4 0.1 broadcast_in_dim.10
  1.5 14.5 %all_to_all.30 = bf16[8,2,4096]{2,1,0:T(2,128)(2,1)S(1)} all-to-all(bf16[8,2,4096]{2,1,0:T(2,128)(2,1)S(1)} %broadcast_in_dim.10), channel_id=1, replica_groups=mesh['blk'=8,'side'=2,'half'=2] {'blk'}, dimensions={0} | all-to-all | bytes 262144 | tf_op jit(solution)/shard_map/all_to_all | solution.py:140
  15.9 0.1 reshape.40.mine_ref
  16.0 0.1 collective-permute-start
  16.1 0.8 dynamic_update_slice.3.base_ref
  16.9 0.0 copy-start.1
  16.9 0.5 collective-permute-done.other_ref
  17.4 15.4 %head_step.3 = (f32[16,4096]{1,0:T(8,128)S(1)}, f32[16,4096]{1,0:T(8,128)S(1)}, f32[8,128]{1,0:T(8,128)S(1)}) custom-call(bf16[16,4096]{1,0:T(8,128)(2,1)S(1)} %reshape.40.mine_ref, bf16[16,4096]{1,0:T(8,128)(2,1)S(1)} %collective-permute-done.other_ref, f32[8,128]{1,0:T(8,128)S(1)} %dynamic_update_slice.3.base_ref, bf16[1792,4096]{1,0:T(8,128)(2,1)} %w1_ref.5, ...), custom_call_target="tpu_custom_call" | custom-call | flops 1409286144 | bytes 22020096 | tf_op jit(solution)/shard_map/head_step/pallas_call | solution.py:104
  32.9 0.2 collective-permute-start.1
  33.1 1.4 collective-permute-done.1
  34.5 0.2 reshape.41
  34.6 11.9 %all_to_all.31 = f32[8,2,4096]{2,1,0:T(2,128)S(1)} all-to-all(f32[8,2,4096]{2,1,0:T(2,128)S(1)} %reshape.41), channel_id=1, replica_groups=mesh['blk'=8,'side'=2,'half'=2] {'blk'}, dimensions={0} | all-to-all | bytes 524288 | tf_op jit(solution)/shard_map/all_to_all | solution.py:140
  46.6 0.1 reduce_sum.45
  46.7 0.1 fusion.6
  46.7 0.1 broadcast_in_dim.13
  46.8 10.7 %all_to_all.32 = bf16[8,2,4096]{2,1,0:T(2,128)(2,1)S(1)} all-to-all(bf16[8,2,4096]{2,1,0:T(2,128)(2,1)S(1)} %broadcast_in_dim.13), channel_id=1, replica_groups=mesh['blk'=8,'side'=2,'half'=2] {'blk'}, dimensions={0} | all-to-all | bytes 262144 | tf_op jit(solution)/shard_map/all_to_all | solution.py:140
  57.5 0.1 reshape.42.mine_ref
  57.6 0.1 collective-permute-start.2
  57.7 1.3 collective-permute-done.2.other_ref
  59.0 15.4 %head_step.4 = (f32[16,4096]{1,0:T(8,128)S(1)}, f32[16,4096]{1,0:T(8,128)S(1)}, f32[8,128]{1,0:T(8,128)S(1)}) custom-call(bf16[16,4096]{1,0:T(8,128)(2,1)S(1)} %reshape.42.mine_ref, bf16[16,4096]{1,0:T(8,128)(2,1)S(1)} %collective-permute-done.2.other_ref, f32[8,128]{1,0:T(8,128)S(1)} %get-tuple-element.13.base_ref, bf16[1792,4096]{1,0:T(8,128)(2,1)} %w1_ref.5, ...), custom_call_target="tpu_custom_call" | custom-call | flops 1409286144 | bytes 22020096 | tf_op jit(solution)/shard_map/head_step/pallas_call | solution.py:104
  74.4 0.2 collective-permute-start.3
  74.7 1.4 collective-permute-done.3
  76.1 0.2 reshape.43
  76.2 11.9 %all_to_all.33 = f32[8,2,4096]{2,1,0:T(2,128)S(1)} all-to-all(f32[8,2,4096]{2,1,0:T(2,128)S(1)} %reshape.43), channel_id=1, replica_groups=mesh['blk'=8,'side'=2,'half'=2] {'blk'}, dimensions={0} | all-to-all | bytes 524288 | tf_op jit(solution)/shard_map/all_to_all | solution.py:140
  88.2 0.1 reduce_sum.46
  88.3 0.1 fusion.5
  88.3 0.1 broadcast_in_dim.28
  88.4 10.7 %all_to_all.34 = bf16[8,2,4096]{2,1,0:T(2,128)(2,1)S(1)} all-to-all(bf16[8,2,4096]{2,1,0:T(2,128)(2,1)S(1)} %broadcast_in_dim.28), channel_id=1, replica_groups=mesh['blk'=8,'side'=2,'half'=2] {'blk'}, dimensions={0} | all-to-all | bytes 262144 | tf_op jit(solution)/shard_map/all_to_all | solution.py:140
  99.1 0.1 reshape.44.mine_ref
  99.2 0.1 collective-permute-start.4
  99.2 1.3 collective-permute-done.4.other_ref
  100.6 15.9 %head_step.5 = (f32[16,4224]{1,0:T(8,128)S(1)}, f32[16,4224]{1,0:T(8,128)S(1)}, f32[8,128]{1,0:T(8,128)}) custom-call(bf16[16,4096]{1,0:T(8,128)(2,1)S(1)} %reshape.44.mine_ref, bf16[16,4096]{1,0:T(8,128)(2,1)S(1)} %collective-permute-done.4.other_ref, f32[8,128]{1,0:T(8,128)S(1)} %get-tuple-element.16.base_ref, bf16[1792,4096]{1,0:T(8,128)(2,1)} %w1_ref.5, ...), custom_call_target="tpu_custom_call" | custom-call | flops 1409286144 | bytes 22020096 | tf_op jit(solution)/shard_map/head_step/pallas_call | solution.py:104
  116.5 0.2 collective-permute-start.5
  116.7 1.4 collective-permute-done.5
  118.1 0.9 reshape.45
  119.0 3.4 %all-to-all-start.5 = ((f32[8,2,4224]{2,1,0:T(2,128)}), f32[8,2,4224]{2,1,0:T(2,128)S(1)}, u32[]{:S(2)}, u32[]{:S(2)}) async-start(f32[8,2,4224]{2,1,0:T(2,128)} %reshape.45), calls=%async_computation.5 | async-start | bytes 540672 | tf_op jit(solution)/shard_map/all_to_all | solution.py:140
  122.4 9.6 %all-to-all-done.5 = f32[8,2,4224]{2,1,0:T(2,128)S(1)} async-done(((f32[8,2,4224]{2,1,0:T(2,128)}), f32[8,2,4224]{2,1,0:T(2,128)S(1)}, u32[]{:S(2)}, u32[]{:S(2)}) %all-to-all-start.5) | async-done | bytes 270368 | tf_op jit(solution)/shard_map/all_to_all | solution.py:140
  132.0 0.1 reduce_sum.47
  132.1 0.6 slice_reduce_fusion
  132.7 1.3 exponential_reduce_fusion
  134.0 0.7 fusion.2
  134.7 1.4 pad_maximum_fusion
  136.1 1.5 %collective-permute-start.6 = (f32[2]{0:T(128)S(1)}, f32[2]{0:T(128)S(1)}, u32[]{:S(2)}, u32[]{:S(2)}) collective-permute-start(f32[2]{0:T(128)S(1)} %pad_maximum_fusion), channel_id=1, source_target_pairs={{0,2},{2,0},{1,3},{3,1},{4,6},{6,4},{5,7},{7,5},{8,10},{10,8},{9,1... | collective-permute-start | bytes 32 | tf_op jit(solution)/shard_map/ppermute | solution.py:169
  137.6 0.6 dynamic-slice_bitcast_fusion
  138.1 1.5 %collective-permute-done.6 = f32[2]{0:T(128)S(1)} collective-permute-done((f32[2]{0:T(128)S(1)}, f32[2]{0:T(128)S(1)}, u32[]{:S(2)}, u32[]{:S(2)}) %collective-permute-start.6) | collective-permute-done | bytes 40 | tf_op jit(solution)/shard_map/ppermute | solution.py:169
  139.6 0.6 fusion.7
  141.5 3.3 %fusion.3 = f32[]{:T(128)} fusion(f32[1]{0:T(128)} %get-tuple-element.23, f32[1]{0:T(128)} %bitcast.6, f32[1]{0:T(128)} %get-tuple-element.24, f32[1]{0:T(128)} %bitcast.5, f32[]{:T(128)S(6)} %reduce_max.20), kind=kLoop, calls=%fused_computation.10 | loop fusion | flops 9 | bytes 24 | tf_op jit(solution)/shard_map/reduce_sum | solution.py:173
  (8 shorter events, 0.1 us)
Async XLA Ops:
  16.0 1.4 collective-permute-start
  16.9 29.8 %copy-start = (f32[2,4096]{1,0:T(2,128)S(1)}, f32[2,4096]{1,0:T(2,128)}, u32[]{:S(2)}) copy-start(f32[2,4096]{1,0:T(2,128)} %param.6) | copy-start | bytes 98308
  16.9 29.8 %copy-start.1 = (bf16[3,2,4096]{2,1,0:T(2,128)(2,1)S(1)}, bf16[3,2,4096]{2,1,0:T(2,128)(2,1)}, u32[]{:S(2)}) copy-start(bf16[3,2,4096]{2,1,0:T(2,128)(2,1)} %param.8) | copy-start | bytes 147460
  32.9 1.6 %collective-permute-start.1 = (f32[16,4096]{1,0:T(8,128)S(1)}, f32[16,4096]{1,0:T(8,128)S(1)}, u32[]{:S(2)}, u32[]{:S(2)}) collective-permute-start(f32[16,4096]{1,0:T(8,128)S(1)} %get-tuple-element.12), channel_id=1, source_target_pairs={{0,1},{1,0},{2,3},{3,2},{4,5},{5,4},{6,7},{7,6},{8,9},{9,8},{10,11... | collective-permute-start | bytes 786440 | tf_op jit(solution)/shard_map/ppermute | solution.py:143
  57.6 1.4 collective-permute-start.2
  74.4 1.6 %collective-permute-start.3 = (f32[16,4096]{1,0:T(8,128)S(1)}, f32[16,4096]{1,0:T(8,128)S(1)}, u32[]{:S(2)}, u32[]{:S(2)}) collective-permute-start(f32[16,4096]{1,0:T(8,128)S(1)} %get-tuple-element.15), channel_id=1, source_target_pairs={{0,1},{1,0},{2,3},{3,2},{4,5},{5,4},{6,7},{7,6},{8,9},{9,8},{10,11... | collective-permute-start | bytes 786440 | tf_op jit(solution)/shard_map/ppermute | solution.py:143
  99.2 1.4 collective-permute-start.4
  116.5 1.6 %collective-permute-start.5 = (f32[16,4224]{1,0:T(8,128)S(1)}, f32[16,4224]{1,0:T(8,128)S(1)}, u32[]{:S(2)}, u32[]{:S(2)}) collective-permute-start(f32[16,4224]{1,0:T(8,128)S(1)} %get-tuple-element.18), channel_id=1, source_target_pairs={{0,1},{1,0},{2,3},{3,2},{4,5},{5,4},{6,7},{7,6},{8,9},{9,8},{10,11... | collective-permute-start | bytes 811016 | tf_op jit(solution)/shard_map/ppermute | solution.py:143
  119.0 13.0 %all-to-all-start.5 = ((f32[8,2,4224]{2,1,0:T(2,128)}), f32[8,2,4224]{2,1,0:T(2,128)S(1)}, u32[]{:S(2)}, u32[]{:S(2)}) async-start(f32[8,2,4224]{2,1,0:T(2,128)} %reshape.45), calls=%async_computation.5 | async-start | bytes 540672 | tf_op jit(solution)/shard_map/all_to_all | solution.py:140
  136.1 3.6 %collective-permute-start.6 = (f32[2]{0:T(128)S(1)}, f32[2]{0:T(128)S(1)}, u32[]{:S(2)}, u32[]{:S(2)}) collective-permute-start(f32[2]{0:T(128)S(1)} %pad_maximum_fusion), channel_id=1, source_target_pairs={{0,2},{2,0},{1,3},{3,1},{4,6},{6,4},{5,7},{7,5},{8,10},{10,8},{9,1... | collective-permute-start | bytes 32 | tf_op jit(solution)/shard_map/ppermute | solution.py:169
where the time goes:
time: 147 us
  blocking collectives  59.7 us (41%)
  Pallas kernels  46.8 us (32%)
  waiting for transfers between devices  18.4 us (13%)
  other arithmetic  8.49 us (6%)
  starting transfers between devices  5.76 us (4%)
  between operations  3.92 us (3%)
  local copies, waits for them, and re-layouts  3.49 us (2%)
    all_to_all x5, blocking collectives, exchange(): return lax.all_to_all(value, 'blk', 0, 0, tiled=True)  59.7 us
    pallas_call x3, Pallas kernels, head_step(): pl.pallas_call(functools.partial(step_kernel, last=last, steps=steps), ou...  46.8 us
    all_to_all x1, waiting for transfers between devices, exchange(): return lax.all_to_all(value, 'blk', 0, 0, tiled=True)  9.57 us
    ppermute x6, waiting for transfers between devices, swap(): return lax.ppermute(value, 'half', [(0, 1), (1, 0)])  7.35 us
    all_to_all x1, starting transfers between devices, exchange(): return lax.all_to_all(value, 'blk', 0, 0, tiled=True)  3.41 us
    reduce_sum x1, other arithmetic, per_device(): total = jnp.sum(totals * jnp.exp(tops - top))  3.27 us
  transfers between devices with their start and end apart: 8, of which 8 were waited for; matrix products, arithmetic and copies ran while one was open for 1% of the time, Pallas kernels for 0%

commit v1 on v0

v1 whole, which is shorter than its diff:
```python
import functools
import math

import jax
import jax.numpy as jnp
from jax import lax
from jax.experimental import pallas as pl
from jax.experimental.pallas import tpu as pltpu
from jax.sharding import Mesh
from jax.sharding import PartitionSpec as P

LANES = 128
GRANT = 16 * 1024 * 1024


def chunk_rows(rows):
    return 128 if rows % 128 == 0 else rows


def column_tile(columns):
    return 512 if columns % 512 == 0 else columns


def lane_width(count):
    return -(-count // LANES) * LANES


def stack_rows(mine_ref, other_ref, rows_ref):
    peers, own = mine_ref.shape[0], mine_ref.shape[1]
    for k, ref in enumerate((mine_ref, other_ref)):
        for d in range(peers):
            rows_ref[pl.ds((k * peers + d) * own, own), :] = ref[d].astype(jnp.float32)
    return rows_ref[...].astype(jnp.bfloat16)


def put_rows(out, cols, rows):
    own = out.shape[1]
    for d in range(out.shape[0]):
        out[d, :, cols] = rows[d * own : (d + 1) * own]


def as_row(column, width):
    spread = jnp.broadcast_to(column, (column.shape[0], LANES))
    spread = jnp.pad(spread, ((0, width - column.shape[0]), (0, 0)))
    return spread.T[:1, :]


def paired(first, second, rows):
    shape = (rows, first.shape[1])
    odd = lax.broadcasted_iota(jnp.int32, shape, 0) % 2 == 1
    return jnp.where(odd, jnp.broadcast_to(second, shape), jnp.broadcast_to(first, shape))


def factors_of(pre_a, pre_b, pre_c):
    decay = jnp.exp(-jnp.abs(pre_a))
    soft = jnp.maximum(pre_a, 0.0) + jnp.log1p(decay)
    sigma = jnp.where(pre_a >= 0.0, 1.0, decay) / (1.0 + decay)
    tan_b = jnp.tanh(pre_b)
    soft_tan = soft * tan_b
    return (
        jnp.sum(soft_tan * pre_c, axis=1, keepdims=True),
        (sigma * tan_b * pre_c).astype(jnp.bfloat16),
        (soft * (1.0 - tan_b * tan_b) * pre_c).astype(jnp.bfloat16),
        soft_tan.astype(jnp.bfloat16),
    )


def project(state, held, i, rows):
    contract = (((1,), (1,)), ((), ()))
    return lax.dot_general(state, held[i, rows], contract, preferred_element_type=jnp.float32)


def finish(energy, base_ref, mine_out, other_out, next_base, held, factors, last, steps):
    near, columns = mine_out.shape[0] * mine_out.shape[1], held.shape[2]
    width = base_ref.shape[1]
    shift = energy / steps
    mine_row = base_ref[0:1, :] - as_row(shift[:near], width)
    other_row = base_ref[1:2, :] - as_row(shift[near:], width)
    if last:
        tail = pl.ds(columns, width)
        put_rows(mine_out, tail, paired(mine_row, other_row, near))
        put_rows(other_out, tail, paired(other_row, mine_row, near))
    next_base[...] = paired(mine_row, other_row, 8)
    tile = column_tile(columns)
    for j in range(columns // tile):
        cols = pl.ds(j * tile, tile)
        total = jnp.dot(factors[0], held[0, :, cols], preferred_element_type=jnp.float32)
        total = total + jnp.dot(factors[1], held[1, :, cols], preferred_element_type=jnp.float32)
        total = total + jnp.dot(factors[2], held[2, :, cols], preferred_element_type=jnp.float32)
        put_rows(mine_out, cols, total[:near])
        put_rows(other_out, cols, total[near:])


def first_kernel(
    mine_ref, other_ref, base_ref, w1_ref, w2_ref, w3_ref,
    mine_out, other_out, next_base, held, rows_ref, factors, sems, *, last, steps,
):
    hidden = held.shape[1]
    chunk = chunk_rows(hidden)
    start = lax.axis_index("half") * hidden
    sources = (w1_ref, w2_ref, w3_ref)
    copies = []
    for j in range(hidden // chunk):
        for i in range(3):
            copy = pltpu.make_async_copy(
                sources[i].at[pl.ds(pl.multiple_of(start + j * chunk, 16), chunk)],
                held.at[i, pl.ds(j * chunk, chunk)],
                sems.at[j, i],
            )
            copy.start()
            copies.append(copy)
    state = stack_rows(mine_ref, other_ref, rows_ref)
    energy = jnp.zeros((state.shape[0], 1), jnp.float32)
    for j in range(hidden // chunk):
        rows = pl.ds(j * chunk, chunk)
        for i in range(3):
            copies[3 * j + i].wait()
        share, *found = factors_of(*(project(state, held, i, rows) for i in range(3)))
        energy = energy + share
        for i in range(3):
            factors[i, :, rows] = found[i]
    finish(energy, base_ref, mine_out, other_out, next_base, held, factors, last, steps)


def later_kernel(
    mine_ref, other_ref, base_ref, held, mine_out, other_out, next_base, rows_ref, factors,
    *, last, steps,
):
    state = stack_rows(mine_ref, other_ref, rows_ref)
    every = pl.ds(0, held.shape[1])
    energy, *found = factors_of(*(project(state, held, i, every) for i in range(3)))
    for i in range(3):
        factors[i] = found[i]
    finish(energy, base_ref, mine_out, other_out, next_base, held, factors, last, steps)


def head_step(mine, other, base, weights, held, hidden, last, steps):
    peers, own, columns = mine.shape
    near = peers * own
    width = base.shape[1]
    chunk = chunk_rows(hidden)
    wide = columns + width if last else columns
    vmem = pl.BlockSpec(memory_space=pltpu.VMEM)
    results = [
        jax.ShapeDtypeStruct((peers, own, wide), jnp.float32),
        jax.ShapeDtypeStruct((peers, own, wide), jnp.float32),
        jax.ShapeDtypeStruct((8, width), jnp.float32),
    ]
    scratch = [
        pltpu.VMEM((2 * near, columns), jnp.float32),
        pltpu.VMEM((3, 2 * near, hidden), jnp.bfloat16),
    ]
    if held is None:
        kernel = first_kernel
        sources = tuple(pltpu.with_memory_space_constraint(w, pltpu.HBM) for w in weights)
        specs = [pl.BlockSpec(memory_space=pltpu.HBM)] * 3
        results.append(pltpu.VMEM((3, hidden, columns), jnp.bfloat16))
        scratch.append(pltpu.SemaphoreType.DMA((hidden // chunk, 3)))
    else:
        kernel, specs = later_kernel, [vmem]
        sources = (pltpu.with_memory_space_constraint(held, pltpu.VMEM),)
    return pl.pallas_call(
        functools.partial(kernel, last=last, steps=steps),
        out_shape=tuple(results),
        in_specs=[vmem] * 3 + specs,
        out_specs=(vmem,) * len(results),
        scratch_shapes=scratch,
        compiler_params=pltpu.CompilerParams(vmem_limit_bytes=GRANT),
        cost_estimate=pl.CostEstimate(
            flops=24 * near * hidden * columns,
            bytes_accessed=6 * hidden * columns,
            transcendentals=8 * near * hidden,
        ),
        name="head_step",
    )(mine, other, base, *sources)


def update_kernel(got_ref, state_ref, noise_ref, state_out, second_out, *, step, steps):
    own, columns = state_ref.shape
    got = got_ref[0]
    for d in range(1, got_ref.shape[0]):
        got = got + got_ref[d]
    beta = (step + 1) / steps
    state = state_ref[...]
    state = (
        state
        - 0.05 * (state + beta * got[:, :columns])
        + math.sqrt(0.1) * noise_ref[step].astype(jnp.float32)
    )
    state_out[...] = state
    if step < steps - 1:
        rounded = state.astype(jnp.bfloat16)
        for d in range(second_out.shape[0]):
            second_out[d] = rounded
        return
    near = got_ref.shape[0] * own
    width = got.shape[1] - columns
    plane = got[:, columns:]
    inside = lax.broadcasted_iota(jnp.int32, plane.shape, 1) < near
    valid = jnp.where(inside, plane, -jnp.inf)
    top = jnp.max(jnp.max(valid, axis=1, keepdims=True), axis=0, keepdims=True)
    shares = jnp.sum(jnp.exp(valid - top), axis=1, keepdims=True)
    total = jnp.sum(shares, axis=0, keepdims=True)
    shape = second_out.shape
    row = lax.broadcasted_iota(jnp.int32, shape, 0)
    at = lax.axis_index("blk") * own
    mine = pltpu.roll(jnp.broadcast_to(plane[0:1, :], shape), (width - at) % width, 1)
    second_out[...] = jnp.where(row == 0, top, jnp.where(row == 1, total, mine))


def update(got, state, noise, step):
    steps = noise.shape[0]
    vmem = pl.BlockSpec(memory_space=pltpu.VMEM)
    if step < steps - 1:
        second = jax.ShapeDtypeStruct((got.shape[0],) + state.shape, jnp.bfloat16)
    else:
        second = jax.ShapeDtypeStruct((8, got.shape[2] - state.shape[1]), jnp.float32)
    return pl.pallas_call(
        functools.partial(update_kernel, step=step, steps=steps),
        out_shape=(jax.ShapeDtypeStruct(state.shape, jnp.float32), second),
        in_specs=[vmem] * 3,
        out_specs=(vmem, vmem),
        compiler_params=pltpu.CompilerParams(vmem_limit_bytes=GRANT),
        name="update",
    )(got, state, noise)


def merge_kernel(*refs, chains):
    out_ref = refs[-1]
    top = refs[0][0:1, :LANES]
    for ref in refs[1:-1]:
        top = jnp.maximum(top, ref[0:1, :LANES])
    total = jnp.zeros_like(top)
    for ref in refs[:-1]:
        total = total + ref[1:2, :LANES] * jnp.exp(ref[0:1, :LANES] - top)
    out_ref[...] = top + jnp.log(total) - math.log(chains)


def merge(blocks, chains):
    vmem = pl.BlockSpec(memory_space=pltpu.VMEM)
    return pl.pallas_call(
        functools.partial(merge_kernel, chains=chains),
        out_shape=jax.ShapeDtypeStruct((1, LANES), jnp.float32),
        in_specs=[vmem] * len(blocks),
        out_specs=vmem,
        compiler_params=pltpu.CompilerParams(vmem_limit_bytes=1 << 20),
        name="merge",
    )(*blocks)


def per_device(start_state, start_log_weight, noise, first_weight, second_weight, third_weight):
    steps = noise.shape[0]
    own, columns = start_state.shape
    weights = (first_weight, second_weight, third_weight)
    peers, halves, planes = lax.axis_size("blk"), lax.axis_size("half"), lax.axis_size("side")
    assert halves == 2
    hidden = first_weight.shape[0] // halves
    near = peers * own
    width = lane_width(near)
    at = lax.axis_index("blk") * own

    def exchange(value):
        return lax.all_to_all(value, "blk", 0, 0, tiled=True)

    def swap(value):
        return lax.ppermute(value, "half", [(0, 1), (1, 0)])

    base = lax.dynamic_update_slice(jnp.zeros((8, width), jnp.float32), start_log_weight[None], (0, at))
    state, held = start_state, None
    copies = jnp.broadcast_to(state.astype(jnp.bfloat16)[None], (peers, own, columns))
    for step in range(steps):
        last = step == steps - 1
        mine = exchange(copies)
        other = swap(mine)
        mine_part, other_part, base, *kept = head_step(mine, other, base, weights, held, hidden, last, steps)
        held = kept[0] if kept else held
        state, copies = update(exchange(mine_part + swap(other_part)), state, noise, step)
    block = copies
    blocks = [block]
    for shift in range(1, planes):
        blocks.append(lax.ppermute(block, "side", [(a, (a + shift) % planes) for a in range(planes)]))
    log_weight = block[2, :own]
    log_ratio = merge(blocks, near * halves * planes)[0, 0]
    return (state, log_weight, log_ratio)


def solution(mesh):
    blk, grp = mesh.shape["blk"], mesh.shape["grp"]
    fine = Mesh(mesh.devices.reshape(blk, grp // 2, 2), ("blk", "side", "half"))
    every = ("blk", "side", "half")
    placed = (
        P(every, None),
        P(every),
        P(None, every, None),
        P("blk", None),
        P("blk", None),
        P("blk", None),
    )
    return jax.shard_map(
        per_device,
        mesh=fine,
        in_specs=placed,
        out_specs=(P(every, None), P(every), P()),
        check_vma=False,
    )
```

time: 147 us -> 126 us (0.86)
  blocking collectives: 59.7 us -> 72.6 us
  waiting for transfers between devices: 18.4 us -> 9.03 us
  Pallas kernels: 46.8 us -> 38.3 us
  other arithmetic: 8.49 us -> 1.19 us
  starting transfers between devices: 5.76 us -> 2.07 us
  between operations: 3.92 us -> 0.7 us
  local copies, waits for them, and re-layouts: 3.49 us -> 1.35 us
    all_to_all x5 -> x6, blocking collectives: 59.7 us -> 72.6 us  [exchange(): return lax.all_to_all(value, 'blk', 0, 0, tiled=True)]
    all_to_all x1 -> x0, waiting for transfers between devices: 9.57 us -> none  [exchange(): return lax.all_to_all(value, 'blk', 0, 0, tiled=True)]
    pallas_call x3 -> x7, Pallas kernels: 46.8 us -> 38.3 us  [the longest x3 37 us: head_step(): pl.pallas_call(functools.partial(kernel, last=last, steps=steps), out_sha...]
    reduce_sum x5 -> x0, other arithmetic: 4.87 us -> none  [the longest x1 3.27 us: per_device(): total = jnp.sum(totals * jnp.exp(tops - top))]
    all_to_all x1 -> x0, starting transfers between devices: 3.41 us -> none  [exchange(): return lax.all_to_all(value, 'blk', 0, 0, tiled=True)]
  transfers between devices with their start and end apart: 8 -> 7, of which waited for: 8 -> 7; matrix products, arithmetic and copies ran while one was open for 1% -> 1% of each run, Pallas kernels for 0% -> 0%
where the time goes in v1:
time: 126 us; the launch traced here: 125 us
  blocking collectives  72.6 us (58%)
  Pallas kernels  38.3 us (30%)
  waiting for transfers between devices  9.03 us (7%)
  starting transfers between devices  2.07 us (2%)
  local copies, waits for them, and re-layouts  1.35 us (1%)
    all_to_all x6, blocking collectives, exchange(): return lax.all_to_all(value, 'blk', 0, 0, tiled=True)  72.6 us
    pallas_call x3, Pallas kernels, head_step(): pl.pallas_call(functools.partial(kernel, last=last, steps=steps), out_sha...  37 us
    ppermute x6, waiting for transfers between devices, swap(): return lax.ppermute(value, 'half', [(0, 1), (1, 0)])  7.43 us
  transfers between devices with their start and end apart: 7, of which 7 were waited for; matrix products, arithmetic and copies ran while one was open for 1% of the time, Pallas kernels for 0%

profile of v1, /device:TPU:0, one launch (start us, length us, event | category | flops | bytes accessed | tf_op | source)
XLA Modules:
  0.0 125.3 jit_solution(6032656653423245172)
XLA Ops:
  0.6 0.8 convert_element_type.3
  1.4 0.1 broadcast_in_dim.12
  1.5 14.5 %all_to_all.30.mine_ref = bf16[8,2,4096]{2,1,0:T(2,128)(2,1)S(1)} all-to-all(bf16[8,2,4096]{2,1,0:T(2,128)(2,1)S(1)} %broadcast_in_dim.12), channel_id=1, replica_groups=mesh['blk'=8,'side'=2,'half'=2] {'blk'}, dimensions={0} | all-to-all | bytes 262144 | tf_op jit(solution)/shard_map/all_to_all | solution.py:263
  15.9 0.0 collective-permute-start
  15.9 0.8 dynamic_update_slice.3.base_ref
  16.7 0.0 copy-start
  16.7 0.0 copy-start.1
  16.7 0.6 collective-permute-done.other_ref
  17.3 15.5 %head_step.3 = (f32[8,2,4096]{2,1,0:T(2,128)S(1)}, f32[8,2,4096]{2,1,0:T(2,128)S(1)}, f32[8,128]{1,0:T(8,128)S(1)}, bf16[3,896,4096]{2,1,0:T(8,128)(2,1)S(1)}) custom-call(bf16[8,2,4096]{2,1,0:T(2,128)(2,1)S(1)} %all_to_all.30.mine_ref, bf16[8,2,4096]{2,1,0:T(2,128)(2,1)S(1)} %collective-permute-done.other_ref, f32[8,128]{1,0:T(8,128)S(1)} %dynamic_update_slice.3.base_ref, ...), custom_call_target="tpu_custom_call" | custom-call | flops 1409286144 | bytes 22020096 | tf_op jit(solution)/shard_map/head_step/pallas_call | solution.py:162
  32.8 0.2 collective-permute-start.1
  33.0 1.4 %collective-permute-done.1 = f32[8,2,4096]{2,1,0:T(2,128)S(1)} collective-permute-done((f32[8,2,4096]{2,1,0:T(2,128)S(1)}, f32[8,2,4096]{2,1,0:T(2,128)S(1)}, u32[]{:S(2)}, u32[]{:S(2)}) %collective-permute-start.1) | collective-permute-done | bytes 262176 | tf_op jit(solution)/shard_map/ppermute | solution.py:266
  34.4 0.1 add.13
  34.6 11.9 %all_to_all.31.got_ref = f32[8,2,4096]{2,1,0:T(2,128)S(1)} all-to-all(f32[8,2,4096]{2,1,0:T(2,128)S(1)} %add.13), channel_id=1, replica_groups=mesh['blk'=8,'side'=2,'half'=2] {'blk'}, dimensions={0} | all-to-all | bytes 524288 | tf_op jit(solution)/shard_map/all_to_all | solution.py:263
  46.5 0.0 copy-done
  46.5 0.0 copy-done.1
  46.5 10.7 %all_to_all.32.mine_ref = bf16[8,2,4096]{2,1,0:T(2,128)(2,1)S(1)} all-to-all(bf16[8,2,4096]{2,1,0:T(2,128)(2,1)S(1)} %get-tuple-element.20), channel_id=1, replica_groups=mesh['blk'=8,'side'=2,'half'=2] {'blk'}, dimensions={0} | all-to-all | bytes 262144 | tf_op jit(solution)/shard_map/all_to_all | solution.py:263
  57.3 0.0 collective-permute-start.2
  57.3 1.3 %collective-permute-done.2.other_ref = bf16[8,2,4096]{2,1,0:T(2,128)(2,1)S(1)} collective-permute-done((bf16[8,2,4096]{2,1,0:T(2,128)(2,1)S(1)}, bf16[8,2,4096]{2,1,0:T(2,128)(2,1)S(1)}, u32[]{:S(2)}, u32[]{:S(2)}) %collective-permute-start.2) | collective-permute-done | bytes 131104 | tf_op jit(solution)/shard_map/ppermute | solution.py:266
  58.6 10.5 %head_step.4 = (f32[8,2,4096]{2,1,0:T(2,128)S(1)}, f32[8,2,4096]{2,1,0:T(2,128)S(1)}, f32[8,128]{1,0:T(8,128)S(1)}) custom-call(bf16[8,2,4096]{2,1,0:T(2,128)(2,1)S(1)} %all_to_all.32.mine_ref, bf16[8,2,4096]{2,1,0:T(2,128)(2,1)S(1)} %collective-permute-done.2.other_ref, f32[8,128]{1,0:T(8,128)S(1)} %get-tuple-element.21.base_ref, ...), custom_call_target="tpu_custom_call" | custom-call | flops 1409286144 | bytes 22020096 | tf_op jit(solution)/shard_map/head_step/pallas_call | solution.py:162
  69.1 0.2 collective-permute-start.3
  69.3 1.4 %collective-permute-done.3 = f32[8,2,4096]{2,1,0:T(2,128)S(1)} collective-permute-done((f32[8,2,4096]{2,1,0:T(2,128)S(1)}, f32[8,2,4096]{2,1,0:T(2,128)S(1)}, u32[]{:S(2)}, u32[]{:S(2)}) %collective-permute-start.3) | collective-permute-done | bytes 262176 | tf_op jit(solution)/shard_map/ppermute | solution.py:266
  70.7 0.1 add.14
  70.8 11.9 %all_to_all.33.got_ref = f32[8,2,4096]{2,1,0:T(2,128)S(1)} all-to-all(f32[8,2,4096]{2,1,0:T(2,128)S(1)} %add.14), channel_id=1, replica_groups=mesh['blk'=8,'side'=2,'half'=2] {'blk'}, dimensions={0} | all-to-all | bytes 524288 | tf_op jit(solution)/shard_map/all_to_all | solution.py:263
  82.8 10.7 %all_to_all.34.mine_ref = bf16[8,2,4096]{2,1,0:T(2,128)(2,1)S(1)} all-to-all(bf16[8,2,4096]{2,1,0:T(2,128)(2,1)S(1)} %get-tuple-element.26), channel_id=1, replica_groups=mesh['blk'=8,'side'=2,'half'=2] {'blk'}, dimensions={0} | all-to-all | bytes 262144 | tf_op jit(solution)/shard_map/all_to_all | solution.py:263
  93.5 0.0 collective-permute-start.4
  93.5 1.3 %collective-permute-done.4.other_ref = bf16[8,2,4096]{2,1,0:T(2,128)(2,1)S(1)} collective-permute-done((bf16[8,2,4096]{2,1,0:T(2,128)(2,1)S(1)}, bf16[8,2,4096]{2,1,0:T(2,128)(2,1)S(1)}, u32[]{:S(2)}, u32[]{:S(2)}) %collective-permute-start.4) | collective-permute-done | bytes 131104 | tf_op jit(solution)/shard_map/ppermute | solution.py:266
  94.9 11.0 %head_step.5 = (f32[8,2,4224]{2,1,0:T(2,128)S(1)}, f32[8,2,4224]{2,1,0:T(2,128)S(1)}, f32[8,128]{1,0:T(8,128)}) custom-call(bf16[8,2,4096]{2,1,0:T(2,128)(2,1)S(1)} %all_to_all.34.mine_ref, bf16[8,2,4096]{2,1,0:T(2,128)(2,1)S(1)} %collective-permute-done.4.other_ref, f32[8,128]{1,0:T(8,128)S(1)} %get-tuple-element.27.base_ref, ...), custom_call_target="tpu_custom_call" | custom-call | flops 1409286144 | bytes 22020096 | tf_op jit(solution)/shard_map/head_step/pallas_call | solution.py:162
  105.8 0.1 collective-permute-start.5
  106.0 1.4 %collective-permute-done.5 = f32[8,2,4224]{2,1,0:T(2,128)S(1)} collective-permute-done((f32[8,2,4224]{2,1,0:T(2,128)S(1)}, f32[8,2,4224]{2,1,0:T(2,128)S(1)}, u32[]{:S(2)}, u32[]{:S(2)}) %collective-permute-start.5) | collective-permute-done | bytes 270368 | tf_op jit(solution)/shard_map/ppermute | solution.py:266
  107.4 0.1 add.15
  107.5 12.9 %all_to_all.35.got_ref = f32[8,2,4224]{2,1,0:T(2,128)S(1)} all-to-all(f32[8,2,4224]{2,1,0:T(2,128)S(1)} %add.15), channel_id=1, replica_groups=mesh['blk'=8,'side'=2,'half'=2] {'blk'}, dimensions={0} | all-to-all | bytes 540672 | tf_op jit(solution)/shard_map/all_to_all | solution.py:263
  120.4 0.7 update.5
  121.2 1.5 %collective-permute-start.6 = (f32[8,128]{1,0:T(8,128)S(1)}, f32[8,128]{1,0:T(8,128)S(1)}, u32[]{:S(2)}, u32[]{:S(2)}) collective-permute-start(f32[8,128]{1,0:T(8,128)S(1)} %get-tuple-element.32.refs_0_), channel_id=1, source_target_pairs={{0,2},{2,0},{1,3},{3,1},{4,6},{6,4},{5,7},{7,5},{8,10},{10,8},{9,1... | collective-permute-start | bytes 12296 | tf_op jit(solution)/shard_map/ppermute | solution.py:281
  122.6 0.5 slice_bitcast_fusion
  123.2 1.6 %collective-permute-done.6.refs_1_ = f32[8,128]{1,0:T(8,128)S(1)} collective-permute-done((f32[8,128]{1,0:T(8,128)S(1)}, f32[8,128]{1,0:T(8,128)S(1)}, u32[]{:S(2)}, u32[]{:S(2)}) %collective-permute-start.6) | collective-permute-done | bytes 4128 | tf_op jit(solution)/shard_map/ppermute | solution.py:281
  124.8 0.5 merge.1
  (3 shorter events, 0.1 us)
Async XLA Ops:
  15.9 1.3 %collective-permute-start = (bf16[8,2,4096]{2,1,0:T(2,128)(2,1)S(1)}, bf16[8,2,4096]{2,1,0:T(2,128)(2,1)S(1)}, u32[]{:S(2)}, u32[]{:S(2)}) collective-permute-start(bf16[8,2,4096]{2,1,0:T(2,128)(2,1)S(1)} %all_to_all.30.mine_ref), channel_id=1, source_target_pairs={{0,1},{1,0},{2,3},{3,2},{4,5},{5,4},{6,7},{7,6},{8,9},{9,8},{10,11... | collective-permute-start | bytes 393224 | tf_op jit(solution)/shard_map/ppermute | solution.py:266
  16.7 29.8 %copy-start = (bf16[3,2,4096]{2,1,0:T(2,128)(2,1)S(1)}, bf16[3,2,4096]{2,1,0:T(2,128)(2,1)}, u32[]{:S(2)}) copy-start(bf16[3,2,4096]{2,1,0:T(2,128)(2,1)} %noise_ref.5) | copy-start | bytes 147460
  16.7 29.8 %copy-start.1 = (f32[2,4096]{1,0:T(2,128)S(1)}, f32[2,4096]{1,0:T(2,128)}, u32[]{:S(2)}) copy-start(f32[2,4096]{1,0:T(2,128)} %state_ref.1) | copy-start | bytes 98308
  32.8 1.6 %collective-permute-start.1 = (f32[8,2,4096]{2,1,0:T(2,128)S(1)}, f32[8,2,4096]{2,1,0:T(2,128)S(1)}, u32[]{:S(2)}, u32[]{:S(2)}) collective-permute-start(f32[8,2,4096]{2,1,0:T(2,128)S(1)} %get-tuple-element.19), channel_id=1, source_target_pairs={{0,1},{1,0},{2,3},{3,2},{4,5},{5,4},{6,7},{7,6},{8,9},{9,8},{10,11... | collective-permute-start | bytes 786440 | tf_op jit(solution)/shard_map/ppermute | solution.py:266
  57.3 1.3 %collective-permute-start.2 = (bf16[8,2,4096]{2,1,0:T(2,128)(2,1)S(1)}, bf16[8,2,4096]{2,1,0:T(2,128)(2,1)S(1)}, u32[]{:S(2)}, u32[]{:S(2)}) collective-permute-start(bf16[8,2,4096]{2,1,0:T(2,128)(2,1)S(1)} %all_to_all.32.mine_ref), channel_id=1, source_target_pairs={{0,1},{1,0},{2,3},{3,2},{4,5},{5,4},{6,7},{7,6},{8,9},{9,8},{10,11... | collective-permute-start | bytes 393224 | tf_op jit(solution)/shard_map/ppermute | solution.py:266
  69.1 1.6 %collective-permute-start.3 = (f32[8,2,4096]{2,1,0:T(2,128)S(1)}, f32[8,2,4096]{2,1,0:T(2,128)S(1)}, u32[]{:S(2)}, u32[]{:S(2)}) collective-permute-start(f32[8,2,4096]{2,1,0:T(2,128)S(1)} %get-tuple-element.24), channel_id=1, source_target_pairs={{0,1},{1,0},{2,3},{3,2},{4,5},{5,4},{6,7},{7,6},{8,9},{9,8},{10,11... | collective-permute-start | bytes 786440 | tf_op jit(solution)/shard_map/ppermute | solution.py:266
  93.5 1.3 %collective-permute-start.4 = (bf16[8,2,4096]{2,1,0:T(2,128)(2,1)S(1)}, bf16[8,2,4096]{2,1,0:T(2,128)(2,1)S(1)}, u32[]{:S(2)}, u32[]{:S(2)}) collective-permute-start(bf16[8,2,4096]{2,1,0:T(2,128)(2,1)S(1)} %all_to_all.34.mine_ref), channel_id=1, source_target_pairs={{0,1},{1,0},{2,3},{3,2},{4,5},{5,4},{6,7},{7,6},{8,9},{9,8},{10,11... | collective-permute-start | bytes 393224 | tf_op jit(solution)/shard_map/ppermute | solution.py:266
  105.8 1.5 %collective-permute-start.5 = (f32[8,2,4224]{2,1,0:T(2,128)S(1)}, f32[8,2,4224]{2,1,0:T(2,128)S(1)}, u32[]{:S(2)}, u32[]{:S(2)}) collective-permute-start(f32[8,2,4224]{2,1,0:T(2,128)S(1)} %get-tuple-element.29), channel_id=1, source_target_pairs={{0,1},{1,0},{2,3},{3,2},{4,5},{5,4},{6,7},{7,6},{8,9},{9,8},{10,11... | collective-permute-start | bytes 811016 | tf_op jit(solution)/shard_map/ppermute | solution.py:266
  121.2 3.6 %collective-permute-start.6 = (f32[8,128]{1,0:T(8,128)S(1)}, f32[8,128]{1,0:T(8,128)S(1)}, u32[]{:S(2)}, u32[]{:S(2)}) collective-permute-start(f32[8,128]{1,0:T(8,128)S(1)} %get-tuple-element.32.refs_0_), channel_id=1, source_target_pairs={{0,2},{2,0},{1,3},{3,1},{4,6},{6,4},{5,7},{7,5},{8,10},{10,8},{9,1... | collective-permute-start | bytes 12296 | tf_op jit(solution)/shard_map/ppermute | solution.py:281
